TPU v7x, 32 devices: a whole 2x2x4 slice. The times are simulated.
32 devices in a mesh: section: 8 (over z, x), seq: 4 (over y, core).
Axes of the slice: x: 2, y: 2, z: 4, core: 2. Of those that a mesh axis runs over, the one named last changes fastest.
Arguments:
- held_q: bfloat16 [8, 256, 4096], P('section', None, 'seq'), may hold values from -200 to 200
- held_kv: bfloat16 [8, 256, 4, 256], P('section'), may hold values from -30 to 30
- grad_out: bfloat16 [8, 256, 4096], P('section', None, 'seq'), may hold values from -6 to 6
Outputs:
- grad_q: bfloat16 [8, 256, 4096], P('section', 'seq')
- grad_kv: bfloat16 [8, 256, 4, 256], P('section', 'seq')
All inputs are finite; a program needn't handle non-finite values.
Results may differ from a plain program's by a relative error of at most 0.01.
Values may be sent and summed in bfloat16 or wider, within the bound.
A program may use at most 64 MiB of HBM per device.

v0:
```python
import functools
import math

import jax
import jax.numpy as jnp
from jax import lax
from jax.experimental import pallas as pl
from jax.experimental.pallas import tpu as pltpu
from jax.sharding import PartitionSpec as P

MESH = pl.DeviceIdType.MESH
AHEAD = 3


def dot_last(left, right):
    return lax.dot_general(
        left, right, (((1,), (1,)), ((), ())), preferred_element_type=jnp.float32
    )


def dot_plain(left, right):
    return jnp.dot(left, right, preferred_element_type=jnp.float32)


def kernel(
    n_section,
    n_seq,
    kv_heads,
    head_dim,
    heads,
    block_len,
    held_q,
    held_kv,
    grad_out,
    out_q,
    out_kv,
    q_land,
    kv_all,
    kv_send,
    kv_land,
    g_land,
    key_t,
    dk_acc,
    dv_acc,
    gq_buf,
    kvp_buf,
    kv_slots,
    q_send_sem,
    q_recv_sem,
    kv_send_sem,
    kv_recv_sem,
    g_sem,
    load_sem,
    gq_send_sem,
    gq_recv_sem,
    gq_self_sem,
    kvp_send_sem,
    kvp_recv_sem,
    kvp_self_sem,
):
    section = lax.axis_index("section")
    me = lax.axis_index("seq")
    partner = lax.rem(section + n_section // 2, n_section)
    repeats = n_seq // kv_heads
    own_head = me // repeats
    span = held_q.shape[0]
    tokens = span // n_seq
    scale = head_dim**-0.5

    kv_load = pltpu.make_async_copy(held_kv, kv_all, load_sem)
    kv_load.start()

    def grad_load(h):
        cols = pl.ds(pl.multiple_of(h * head_dim, head_dim), head_dim)
        return pltpu.make_async_copy(grad_out.at[:, cols], g_land.at[h], g_sem.at[h])

    edges = sorted({0, tokens, span}, reverse=True)
    parts = list(zip(edges[1:], edges[:-1]))
    last = heads - 1

    def q_copy(h, part=None):
        cols = pl.ds(pl.multiple_of(h * head_dim, head_dim), head_dim)
        rows = slice(0, span) if part is None else slice(*parts[part])
        slot = h if part is None else last + part
        return pltpu.make_async_remote_copy(
            src_ref=held_q.at[rows, cols],
            dst_ref=q_land.at[h, rows, :],
            send_sem=q_send_sem.at[slot],
            recv_sem=q_recv_sem.at[slot],
            device_id=(partner, me),
            device_id_type=MESH,
        )

    kv_copy = pltpu.make_async_remote_copy(
        src_ref=kv_send,
        dst_ref=kv_land,
        send_sem=kv_send_sem,
        recv_sem=kv_recv_sem,
        device_id=(partner, me),
        device_id_type=MESH,
    )

    barrier = pltpu.get_barrier_semaphore()
    pl.semaphore_signal(barrier, inc=1, device_id=(partner, me), device_id_type=MESH)
    for d in range(1, n_seq):
        peer = lax.rem(me + d, n_seq)
        pl.semaphore_signal(barrier, inc=1, device_id=(section, peer), device_id_type=MESH)
    for h in range(heads):
        grad_load(h).start()
    dk_acc[...] = jnp.zeros_like(dk_acc)
    dv_acc[...] = jnp.zeros_like(dv_acc)
    kv_load.wait()
    for j in range(kv_heads):

        @pl.when(own_head == j)
        def _():
            kv_send[...] = kv_all[:, j, :]

    pl.semaphore_wait(barrier, n_seq)
    kv_copy.start()
    ahead = jnp.where(section >= n_section - n_section // 4, AHEAD, heads)

    def send_unit(unit):
        @pl.when(unit < last)
        def _():
            q_copy(unit).start()

        @pl.when(unit == last)
        def _():
            for part in range(len(parts)):
                q_copy(last, part).start()

    def first_sends(unit, carry):
        @pl.when(unit < ahead)
        def _():
            send_unit(unit)

        return carry

    lax.fori_loop(0, heads, first_sends, 0)

    kv_copy.wait_recv()
    key_t[...] = kv_land[:, :head_dim].astype(jnp.float32).T.astype(jnp.bfloat16)

    def gq_copy(h, d):
        peer = lax.rem(me + d, n_seq)
        col = pl.multiple_of((me * heads + h) * head_dim, head_dim)
        row = pl.multiple_of(peer * tokens, tokens)
        return pltpu.make_async_remote_copy(
            src_ref=gq_buf.at[h, pl.ds(row, tokens), :],
            dst_ref=out_q.at[:, pl.ds(col, head_dim)],
            send_sem=gq_send_sem.at[d - 1, h],
            recv_sem=gq_recv_sem.at[d - 1, h],
            device_id=(section, peer),
            device_id_type=MESH,
        )

    def gq_self(h):
        col = pl.multiple_of((me * heads + h) * head_dim, head_dim)
        row = pl.multiple_of(me * tokens, tokens)
        return pltpu.make_async_copy(
            gq_buf.at[h, pl.ds(row, tokens), :],
            out_q.at[:, pl.ds(col, head_dim)],
            gq_self_sem.at[h],
        )

    def kvp_target():
        if repeats == 1:
            width = 2 * head_dim
            return out_kv.at[:, pl.ds(pl.multiple_of(me * width, width), width)]
        return kv_slots.at[me]

    def kvp_copy(d):
        peer = lax.rem(me + d, n_seq)
        row = pl.multiple_of(peer * tokens, tokens)
        return pltpu.make_async_remote_copy(
            src_ref=kvp_buf.at[pl.ds(row, tokens), :],
            dst_ref=kvp_target(),
            send_sem=kvp_send_sem.at[d - 1],
            recv_sem=kvp_recv_sem.at[d - 1],
            device_id=(section, peer),
            device_id_type=MESH,
        )

    def kvp_self():
        row = pl.multiple_of(me * tokens, tokens)
        return pltpu.make_async_copy(
            kvp_buf.at[pl.ds(row, tokens), :], kvp_target(), kvp_self_sem
        )

    def grads(h, start, stop):
        size = stop - start
        query = q_land[h, start:stop, :]
        grad = g_land[h, start:stop, :]
        score = dot_last(kv_land[:stop, :head_dim], query)
        dprob = dot_last(kv_land[:stop, head_dim:], grad)
        key_pos = lax.broadcasted_iota(jnp.int32, (size, size), 0)
        query_pos = lax.broadcasted_iota(jnp.int32, (size, size), 1)
        diag = jnp.where(key_pos <= query_pos, score[start:], -1e30)
        score = jnp.concatenate([score[:start], diag], axis=0) if start else diag
        top = jnp.max(score, axis=0, keepdims=True)
        expd = jnp.exp2((score - top) * (scale * math.log2(math.e)))
        inverse = 1.0 / jnp.sum(expd, axis=0, keepdims=True)
        prob = expd * inverse
        row_dot = jnp.sum(prob * dprob, axis=0, keepdims=True)
        dscore = (prob * (dprob - row_dot)).astype(jnp.bfloat16)
        weight = prob.astype(jnp.bfloat16)
        dv_acc[:stop, :] += dot_plain(weight, grad)
        dk_acc[:stop, :] += dot_plain(dscore, query)
        gq_t = dot_plain(key_t[:, :stop], dscore) * scale
        gq_buf[h, start:stop, :] = gq_t.T.astype(jnp.bfloat16)

    def send(copy_to, copy_self, start, stop):
        low, high = start // tokens, stop // tokens
        for d in range(1, n_seq):
            peer = lax.rem(me + d, n_seq)

            @pl.when(jnp.logical_and(peer >= low, peer < high))
            def _():
                copy_to(d).start()

        @pl.when(jnp.logical_and(me >= low, me < high))
        def _():
            copy_self().start()

    def send_gq(h, start, stop):
        send(functools.partial(gq_copy, h), functools.partial(gq_self, h), start, stop)

    def send_kvp(start, stop):
        rows = slice(start, stop)
        kvp_buf[rows, :head_dim] = (dk_acc[rows, :] * scale).astype(jnp.bfloat16)
        kvp_buf[rows, head_dim:] = dv_acc[rows, :].astype(jnp.bfloat16)
        send(kvp_copy, kvp_self, start, stop)

    def head_step(h, carry):
        grad_load(h).wait()
        q_copy(h).wait_recv()
        send_unit(h + ahead)
        for start in range(0, span, block_len):
            grads(h, start, start + block_len)
        send_gq(h, 0, span)
        return carry

    lax.fori_loop(0, last, head_step, 0)
    grad_load(last).wait()
    for part, (start, stop) in enumerate(parts):
        q_copy(last, part).wait_recv()
        for low in range(start // block_len * block_len, stop, block_len):
            grads(last, max(low, start), min(low + block_len, stop))
        send_kvp(start, stop)
        send_gq(last, start, stop)

    def drain(h, carry):
        gq_self(h).wait()
        for d in range(1, n_seq):
            gq_copy(h, d).wait()
        return carry

    lax.fori_loop(0, heads, drain, 0)

    def drain_q(h, carry):
        q_copy(h).wait_send()
        return carry

    lax.fori_loop(0, last, drain_q, 0)
    for part in range(len(parts)):
        q_copy(last, part).wait_send()
    kv_copy.wait_send()
    kvp_self().wait()
    for d in range(1, n_seq):
        kvp_copy(d).wait()
    if repeats > 1:
        for j in range(kv_heads):
            total = kv_slots[j * repeats].astype(jnp.float32)
            for i in range(1, repeats):
                total = total + kv_slots[j * repeats + i].astype(jnp.float32)
            width = 2 * head_dim
            out_kv[:, j * width : (j + 1) * width] = total.astype(jnp.bfloat16)


def store_kernel(grad_q, grad_kv, out_q, out_kv, kv_rows, q_sem, kv_sem):
    store_q = pltpu.make_async_copy(grad_q, out_q, q_sem)
    store_q.start()
    width = kv_rows.shape[2]
    for j in range(kv_rows.shape[1]):
        kv_rows[:, j, :] = grad_kv[:, j * width : (j + 1) * width]
    store_kv = pltpu.make_async_copy(kv_rows, out_kv, kv_sem)
    store_kv.start()
    store_q.wait()
    store_kv.wait()


def on_device(n_section, n_seq, held_q, held_kv, grad_out):
    held_q, held_kv, grad_out = held_q[0], held_kv[0], grad_out[0]
    span, width = held_q.shape
    kv_heads = held_kv.shape[1]
    head_dim = held_kv.shape[2] // 2
    heads = width // head_dim
    block_len = min(128, span)
    tokens = span // n_seq
    repeats = n_seq // kv_heads
    bf16 = jnp.bfloat16
    slots = n_seq if repeats > 1 else 1
    hbm = pl.BlockSpec(memory_space=pltpu.HBM)
    vmem = pl.BlockSpec(memory_space=pltpu.VMEM)
    dma = pltpu.SemaphoreType.DMA
    grad_q, grad_kv = pl.pallas_call(
        functools.partial(kernel, n_section, n_seq, kv_heads, head_dim, heads, block_len),
        out_shape=(
            pltpu.VMEM((tokens, n_seq * width), bf16),
            pltpu.VMEM((tokens, kv_heads * 2 * head_dim), bf16),
        ),
        in_specs=[hbm, hbm, hbm],
        out_specs=(vmem, vmem),
        scratch_shapes=[
            pltpu.VMEM((heads, span, head_dim), bf16),
            pltpu.VMEM(held_kv.shape, bf16),
            pltpu.VMEM((span, 2 * head_dim), bf16),
            pltpu.VMEM((span, 2 * head_dim), bf16),
            pltpu.VMEM((heads, span, head_dim), bf16),
            pltpu.VMEM((head_dim, span), bf16),
            pltpu.VMEM((span, head_dim), jnp.float32),
            pltpu.VMEM((span, head_dim), jnp.float32),
            pltpu.VMEM((heads, span, head_dim), bf16),
            pltpu.VMEM((span, 2 * head_dim), bf16),
            pltpu.VMEM((slots, tokens, 2 * head_dim), bf16),
            dma((heads + 2,)),
            dma((heads + 2,)),
            dma,
            dma,
            dma((heads,)),
            dma,
            dma((n_seq - 1, heads)),
            dma((n_seq - 1, heads)),
            dma((heads,)),
            dma((n_seq - 1,)),
            dma((n_seq - 1,)),
            dma,
        ],
        compiler_params=pltpu.CompilerParams(
            collective_id=0, has_side_effects=True, vmem_limit_bytes=63 * 2**20
        ),
    )(held_q, held_kv, grad_out)
    kv_shape = (tokens, kv_heads, 2 * head_dim)
    grad_q, grad_kv = pl.pallas_call(
        store_kernel,
        out_shape=(
            jax.ShapeDtypeStruct(grad_q.shape, bf16),
            jax.ShapeDtypeStruct(kv_shape, bf16),
        ),
        in_specs=[vmem, vmem],
        out_specs=(hbm, hbm),
        scratch_shapes=[pltpu.VMEM(kv_shape, bf16), dma, dma],
        compiler_params=pltpu.CompilerParams(vmem_limit_bytes=4 * 2**20),
    )(grad_q, grad_kv)
    return grad_q[None], grad_kv[None]


def solution(mesh):
    return jax.shard_map(
        functools.partial(on_device, mesh.shape["section"], mesh.shape["seq"]),
        mesh=mesh,
        in_specs=(
            P("section", None, "seq"),
            P("section", None, None, None),
            P("section", None, "seq"),
        ),
        out_specs=(P("section", "seq", None), P("section", "seq", None, None)),
        check_vma=False,
    )
```

profile of v0, /device:TPU:11, one launch (start us, length us, event | category | flops | bytes accessed | tf_op | source)
XLA Modules:
  0.0 38.8 jit_solution(2126747518908447925)
XLA Ops:
  0.6 37.3 %shard_map.50 = (bf16[64,4096]{1,0:T(8,128)(2,1)S(1)}, bf16[64,1024]{1,0:T(8,128)(2,1)S(1)}) custom-call(bf16[256,1024]{1,0:T(8,128)(2,1)} %bitcast.5, bf16[256,4,256]{2,1,0:T(4,128)(2,1)} %bitcast.6, bf16[256,1024]{1,0:T(8,128)(2,1)} %bitcast.7), custom_call_target="tpu_custom_call" | custom-call | tf_op jit(solution)/shard_map/pallas_call | solution.py:307
  38.0 0.9 %shard_map.51 = (bf16[64,4096]{1,0:T(8,128)(2,1)}, bf16[64,4,256]{2,1,0:T(4,128)(2,1)}) custom-call(bf16[64,4096]{1,0:T(8,128)(2,1)S(1)} %get-tuple-element.6.grad_q, bf16[64,1024]{1,0:T(8,128)(2,1)S(1)} %get-tuple-element.7.grad_kv), custom_call_target="tpu_custom_call" | custom-call | tf_op jit(solution)/shard_map/pallas_call | solution.py:345
where the time goes:
time: 39.5 us; the launch traced here: 38.8 us
  Pallas kernels  38.2 us (97%)
  between operations  0.64 us (2%)
    pallas_call x1, Pallas kernels, on_device(): pl.pallas_call(functools.partial(kernel, n_section, n_seq, kv_heads, head...  37.3 us
    pallas_call x1, Pallas kernels, on_device(): pl.pallas_call(store_kernel, out_shape=(jax.ShapeDtypeStruct(grad_q.shape...  0.87 us

commit v1 on v0

--- a/solution.py
+++ b/solution.py
@@ -9,7 +9,7 @@
 from jax.sharding import PartitionSpec as P
 
 MESH = pl.DeviceIdType.MESH
-AHEAD = 3
+AHEAD = 4
 
 
 def dot_last(left, right):
@@ -53,10 +53,9 @@
     load_sem,
     gq_send_sem,
     gq_recv_sem,
-    gq_self_sem,
     kvp_send_sem,
     kvp_recv_sem,
-    kvp_self_sem,
+    door,
 ):
     section = lax.axis_index("section")
     me = lax.axis_index("seq")
@@ -70,9 +69,12 @@
     kv_load = pltpu.make_async_copy(held_kv, kv_all, load_sem)
     kv_load.start()
 
+    def whole(ref, sem):
+        return pltpu.make_async_copy(ref, ref, sem)
+
     def grad_load(h):
         cols = pl.ds(pl.multiple_of(h * head_dim, head_dim), head_dim)
-        return pltpu.make_async_copy(grad_out.at[:, cols], g_land.at[h], g_sem.at[h])
+        return pltpu.make_async_copy(grad_out.at[:, cols], g_land.at[h], g_sem)
 
     edges = sorted({0, tokens, span}, reverse=True)
     parts = list(zip(edges[1:], edges[:-1]))
@@ -85,7 +87,7 @@
         return pltpu.make_async_remote_copy(
             src_ref=held_q.at[rows, cols],
             dst_ref=q_land.at[h, rows, :],
-            send_sem=q_send_sem.at[slot],
+            send_sem=q_send_sem,
             recv_sem=q_recv_sem.at[slot],
             device_id=(partner, me),
             device_id_type=MESH,
@@ -100,15 +102,38 @@
         device_id_type=MESH,
     )
 
+    def send_unit(unit):
+        @pl.when(unit < last)
+        def _():
+            q_copy(unit).start()
+
+        @pl.when(unit == last)
+        def _():
+            for part in range(len(parts)):
+                q_copy(last, part).start()
+
     barrier = pltpu.get_barrier_semaphore()
     pl.semaphore_signal(barrier, inc=1, device_id=(partner, me), device_id_type=MESH)
-    for d in range(1, n_seq):
-        peer = lax.rem(me + d, n_seq)
-        pl.semaphore_signal(barrier, inc=1, device_id=(section, peer), device_id_type=MESH)
+    late = section >= n_section // 2
+    early = jnp.logical_not(late)
+
+    def signal_peers(sem):
+        for d in range(1, n_seq):
+            peer = lax.rem(me + d, n_seq)
+            pl.semaphore_signal(
+                sem, inc=1, device_id=(section, peer), device_id_type=MESH
+            )
+
+    @pl.when(early)
+    def _():
+        signal_peers(barrier)
+
     for h in range(heads):
         grad_load(h).start()
     dk_acc[...] = jnp.zeros_like(dk_acc)
     dv_acc[...] = jnp.zeros_like(dv_acc)
+    pl.semaphore_wait(barrier, jnp.where(early, n_seq, 1))
+    send_unit(0)
     kv_load.wait()
     for j in range(kv_heads):
 
@@ -116,20 +141,9 @@
         def _():
             kv_send[...] = kv_all[:, j, :]
 
-    pl.semaphore_wait(barrier, n_seq)
     kv_copy.start()
     ahead = jnp.where(section >= n_section - n_section // 4, AHEAD, heads)
 
-    def send_unit(unit):
-        @pl.when(unit < last)
-        def _():
-            q_copy(unit).start()
-
-        @pl.when(unit == last)
-        def _():
-            for part in range(len(parts)):
-                q_copy(last, part).start()
-
     def first_sends(unit, carry):
         @pl.when(unit < ahead)
         def _():
@@ -137,8 +151,19 @@
 
         return carry
 
-    lax.fori_loop(0, heads, first_sends, 0)
-
+    lax.fori_loop(1, heads, first_sends, 0)
+
+    @pl.when(early)
+    def _():
+        signal_peers(door)
+        pl.semaphore_wait(door, n_seq - 1)
+        pl.semaphore_signal(door, inc=1, device_id=(partner, me), device_id_type=MESH)
+
+    @pl.when(late)
+    def _():
+        pl.semaphore_wait(door, 1)
+
+    whole(g_land, g_sem).wait()
     kv_copy.wait_recv()
     key_t[...] = kv_land[:, :head_dim].astype(jnp.float32).T.astype(jnp.bfloat16)
 
@@ -149,8 +174,8 @@
         return pltpu.make_async_remote_copy(
             src_ref=gq_buf.at[h, pl.ds(row, tokens), :],
             dst_ref=out_q.at[:, pl.ds(col, head_dim)],
-            send_sem=gq_send_sem.at[d - 1, h],
-            recv_sem=gq_recv_sem.at[d - 1, h],
+            send_sem=gq_send_sem,
+            recv_sem=gq_recv_sem,
             device_id=(section, peer),
             device_id_type=MESH,
         )
@@ -161,7 +186,7 @@
         return pltpu.make_async_copy(
             gq_buf.at[h, pl.ds(row, tokens), :],
             out_q.at[:, pl.ds(col, head_dim)],
-            gq_self_sem.at[h],
+            gq_recv_sem,
         )
 
     def kvp_target():
@@ -176,8 +201,8 @@
         return pltpu.make_async_remote_copy(
             src_ref=kvp_buf.at[pl.ds(row, tokens), :],
             dst_ref=kvp_target(),
-            send_sem=kvp_send_sem.at[d - 1],
-            recv_sem=kvp_recv_sem.at[d - 1],
+            send_sem=kvp_send_sem,
+            recv_sem=kvp_recv_sem,
             device_id=(section, peer),
             device_id_type=MESH,
         )
@@ -185,7 +210,7 @@
     def kvp_self():
         row = pl.multiple_of(me * tokens, tokens)
         return pltpu.make_async_copy(
-            kvp_buf.at[pl.ds(row, tokens), :], kvp_target(), kvp_self_sem
+            kvp_buf.at[pl.ds(row, tokens), :], kvp_target(), kvp_recv_sem
         )
 
     def grads(h, start, stop):
@@ -233,7 +258,6 @@
         send(kvp_copy, kvp_self, start, stop)
 
     def head_step(h, carry):
-        grad_load(h).wait()
         q_copy(h).wait_recv()
         send_unit(h + ahead)
         for start in range(0, span, block_len):
@@ -242,7 +266,6 @@
         return carry
 
     lax.fori_loop(0, last, head_step, 0)
-    grad_load(last).wait()
     for part, (start, stop) in enumerate(parts):
         q_copy(last, part).wait_recv()
         for low in range(start // block_len * block_len, stop, block_len):
@@ -250,25 +273,14 @@
         send_kvp(start, stop)
         send_gq(last, start, stop)
 
-    def drain(h, carry):
-        gq_self(h).wait()
-        for d in range(1, n_seq):
-            gq_copy(h, d).wait()
-        return carry
-
-    lax.fori_loop(0, heads, drain, 0)
-
-    def drain_q(h, carry):
-        q_copy(h).wait_send()
-        return carry
-
-    lax.fori_loop(0, last, drain_q, 0)
-    for part in range(len(parts)):
-        q_copy(last, part).wait_send()
+    away = span - tokens
+    whole(q_land, q_send_sem).wait()
     kv_copy.wait_send()
-    kvp_self().wait()
-    for d in range(1, n_seq):
-        kvp_copy(d).wait()
+    whole(gq_buf.at[:, :away], gq_send_sem).wait()
+    whole(kvp_buf.at[:away], kvp_send_sem).wait()
+    whole(out_q, gq_recv_sem).wait()
+    landed = out_kv if repeats == 1 else kv_slots
+    whole(landed, kvp_recv_sem).wait()
     if repeats > 1:
         for j in range(kv_heads):
             total = kv_slots[j * repeats].astype(jnp.float32)
@@ -324,18 +336,17 @@
             pltpu.VMEM((heads, span, head_dim), bf16),
             pltpu.VMEM((span, 2 * head_dim), bf16),
             pltpu.VMEM((slots, tokens, 2 * head_dim), bf16),
+            dma,
             dma((heads + 2,)),
-            dma((heads + 2,)),
-            dma,
-            dma,
-            dma((heads,)),
-            dma,
-            dma((n_seq - 1, heads)),
-            dma((n_seq - 1, heads)),
-            dma((heads,)),
-            dma((n_seq - 1,)),
-            dma((n_seq - 1,)),
-            dma,
+            dma,
+            dma,
+            dma,
+            dma,
+            dma,
+            dma,
+            dma,
+            dma,
+            pltpu.SemaphoreType.REGULAR,
         ],
         compiler_params=pltpu.CompilerParams(
             collective_id=0, has_side_effects=True, vmem_limit_bytes=63 * 2**20

time: 39.5 us -> 38.4 us (0.972)
  the two profiles are of different devices: /device:TPU:11 before, /device:TPU:26 now
where the time goes in v1:
time: 38.4 us; the launch traced here: 38.3 us
  Pallas kernels  37.6 us (98%)
  between operations  0.64 us (2%)
    pallas_call x1, Pallas kernels, on_device(): pl.pallas_call(functools.partial(kernel, n_section, n_seq, kv_heads, head...  36.8 us
    pallas_call x1, Pallas kernels, on_device(): pl.pallas_call(store_kernel, out_shape=(jax.ShapeDtypeStruct(grad_q.shape...  0.87 us

profile of v1, /device:TPU:26, one launch (start us, length us, event | category | flops | bytes accessed | tf_op | source)
XLA Modules:
  0.0 38.3 jit_solution(2202119557408370530)
XLA Ops:
  0.6 36.8 %shard_map.50 = (bf16[64,4096]{1,0:T(8,128)(2,1)S(1)}, bf16[64,1024]{1,0:T(8,128)(2,1)S(1)}) custom-call(bf16[256,1024]{1,0:T(8,128)(2,1)} %bitcast.5, bf16[256,4,256]{2,1,0:T(4,128)(2,1)} %bitcast.6, bf16[256,1024]{1,0:T(8,128)(2,1)} %bitcast.7), custom_call_target="tpu_custom_call" | custom-call | tf_op jit(solution)/shard_map/pallas_call | solution.py:319
  37.4 0.9 %shard_map.51 = (bf16[64,4096]{1,0:T(8,128)(2,1)}, bf16[64,4,256]{2,1,0:T(4,128)(2,1)}) custom-call(bf16[64,4096]{1,0:T(8,128)(2,1)S(1)} %get-tuple-element.6.grad_q, bf16[64,1024]{1,0:T(8,128)(2,1)S(1)} %get-tuple-element.7.grad_kv), custom_call_target="tpu_custom_call" | custom-call | tf_op jit(solution)/shard_map/pallas_call | solution.py:356

commit v2 on v1

--- a/solution.py
+++ b/solution.py
@@ -9,7 +9,9 @@
 from jax.sharding import PartitionSpec as P
 
 MESH = pl.DeviceIdType.MESH
-AHEAD = 4
+AHEAD = 7
+SHIFT = 4
+SPLIT = 4
 
 
 def dot_last(left, right):
@@ -37,6 +39,7 @@
     q_land,
     kv_all,
     kv_send,
+    kv_help,
     kv_land,
     g_land,
     key_t,
@@ -49,6 +52,8 @@
     q_recv_sem,
     kv_send_sem,
     kv_recv_sem,
+    help_send_sem,
+    help_recv_sem,
     g_sem,
     load_sem,
     gq_send_sem,
@@ -76,41 +81,71 @@
         cols = pl.ds(pl.multiple_of(h * head_dim, head_dim), head_dim)
         return pltpu.make_async_copy(grad_out.at[:, cols], g_land.at[h], g_sem)
 
-    edges = sorted({0, tokens, span}, reverse=True)
-    parts = list(zip(edges[1:], edges[:-1]))
-    last = heads - 1
-
-    def q_copy(h, part=None):
+    half = n_seq // 2
+    upper = me >= half
+    lower = jnp.logical_not(upper)
+    split = min(SPLIT, heads)
+    plain = heads - split
+    middle = span // 2
+    units = heads + split
+    groups = [(0, plain, 0), (plain, split, 1), (heads, split, 2)]
+
+    def first_row(stage):
+        low_rows = upper if stage == 1 else lower
+        return pl.multiple_of(jnp.where(low_rows, 0, middle), middle)
+
+    def q_copy(group, unit):
+        base, _, stage = group
+        h = unit - base + (plain if stage else 0)
         cols = pl.ds(pl.multiple_of(h * head_dim, head_dim), head_dim)
-        rows = slice(0, span) if part is None else slice(*parts[part])
-        slot = h if part is None else last + part
+        rows = pl.ds(first_row(stage), middle) if stage else slice(0, span)
         return pltpu.make_async_remote_copy(
             src_ref=held_q.at[rows, cols],
             dst_ref=q_land.at[h, rows, :],
             send_sem=q_send_sem,
-            recv_sem=q_recv_sem.at[slot],
+            recv_sem=q_recv_sem.at[unit],
             device_id=(partner, me),
             device_id_type=MESH,
         )
 
-    kv_copy = pltpu.make_async_remote_copy(
-        src_ref=kv_send,
-        dst_ref=kv_land,
-        send_sem=kv_send_sem,
-        recv_sem=kv_recv_sem,
-        device_id=(partner, me),
+    shift = span * SHIFT // 256 * 16
+    kept = span - shift
+
+    def kv_copy(rows):
+        return pltpu.make_async_remote_copy(
+            src_ref=kv_send.at[:rows],
+            dst_ref=kv_land.at[:rows],
+            send_sem=kv_send_sem,
+            recv_sem=kv_recv_sem,
+            device_id=(partner, me),
+            device_id_type=MESH,
+        )
+
+    help_copy = pltpu.make_async_remote_copy(
+        src_ref=kv_help,
+        dst_ref=kv_land.at[kept:],
+        send_sem=help_send_sem,
+        recv_sem=help_recv_sem,
+        device_id=(partner, lax.rem(me + half, n_seq)),
         device_id_type=MESH,
     )
 
+    def on_kv(act):
+        @pl.when(upper)
+        def _():
+            act(kv_copy(kept))
+
+        @pl.when(lower)
+        def _():
+            act(kv_copy(span))
+
     def send_unit(unit):
-        @pl.when(unit < last)
-        def _():
-            q_copy(unit).start()
-
-        @pl.when(unit == last)
-        def _():
-            for part in range(len(parts)):
-                q_copy(last, part).start()
+        for group in groups:
+            base, count, _ = group
+
+            @pl.when(jnp.logical_and(unit >= base, unit < base + count))
+            def _():
+                q_copy(group, unit).start()
 
     barrier = pltpu.get_barrier_semaphore()
     pl.semaphore_signal(barrier, inc=1, device_id=(partner, me), device_id_type=MESH)
@@ -141,8 +176,14 @@
         def _():
             kv_send[...] = kv_all[:, j, :]
 
-    kv_copy.start()
-    ahead = jnp.where(section >= n_section - n_section // 4, AHEAD, heads)
+    inner = jnp.logical_and(section >= n_section // 4, section < n_section - n_section // 4)
+    outer = jnp.logical_not(inner)
+
+    @pl.when(jnp.logical_or(outer, upper))
+    def _():
+        on_kv(lambda copy: copy.start())
+
+    ahead = jnp.where(section >= n_section - n_section // 4, AHEAD, units)
 
     def first_sends(unit, carry):
         @pl.when(unit < ahead)
@@ -151,7 +192,17 @@
 
         return carry
 
-    lax.fori_loop(1, heads, first_sends, 0)
+    @pl.when(upper)
+    def _():
+        lax.fori_loop(1, units, first_sends, 0)
+
+    @pl.when(lower)
+    def _():
+        for j in range(kv_heads):
+
+            @pl.when((me + half) // repeats == j)
+            def _():
+                kv_help[...] = kv_all[kept:, j, :]
 
     @pl.when(early)
     def _():
@@ -163,8 +214,23 @@
     def _():
         pl.semaphore_wait(door, 1)
 
+    @pl.when(lower)
+    def _():
+        help_copy.start()
+
+        @pl.when(inner)
+        def _():
+            on_kv(lambda copy: copy.start())
+
+        lax.fori_loop(1, units, first_sends, 0)
+
     whole(g_land, g_sem).wait()
-    kv_copy.wait_recv()
+    on_kv(lambda copy: copy.wait_recv())
+
+    @pl.when(upper)
+    def _():
+        help_copy.wait_recv()
+
     key_t[...] = kv_land[:, :head_dim].astype(jnp.float32).T.astype(jnp.bfloat16)
 
     def gq_copy(h, d):
@@ -257,25 +323,55 @@
         kvp_buf[rows, head_dim:] = dv_acc[rows, :].astype(jnp.bfloat16)
         send(kvp_copy, kvp_self, start, stop)
 
-    def head_step(h, carry):
-        q_copy(h).wait_recv()
-        send_unit(h + ahead)
-        for start in range(0, span, block_len):
-            grads(h, start, start + block_len)
-        send_gq(h, 0, span)
-        return carry
-
-    lax.fori_loop(0, last, head_step, 0)
-    for part, (start, stop) in enumerate(parts):
-        q_copy(last, part).wait_recv()
-        for low in range(start // block_len * block_len, stop, block_len):
-            grads(last, max(low, start), min(low + block_len, stop))
-        send_kvp(start, stop)
-        send_gq(last, start, stop)
+    def rows_step(h, start, stop, done=None):
+        for low in range(start, stop, block_len):
+            grads(h, low, min(low + block_len, stop))
+        if done is not None:
+            done()
+        send_gq(h, start, stop)
+
+    def stage_step(h, stage, final):
+        def after(when, start, stop):
+            def done():
+                @pl.when(jnp.logical_and(final, when))
+                def _():
+                    send_kvp(start, stop)
+
+            return done
+
+        @pl.when(first_row(stage) == 0)
+        def _():
+            rows_step(h, 0, middle, after(stage == 2, 0, middle))
+
+        @pl.when(first_row(stage) == middle)
+        def _():
+            if stage == 1:
+                rows_step(h, middle, span, after(True, middle, span))
+            else:
+                rows_step(h, middle, span, after(True, 0, span))
+
+    for group in groups:
+        base, count, stage = group
+
+        def unit_step(unit, carry):
+            q_copy(group, unit).wait_recv()
+            send_unit(unit + ahead)
+            if stage:
+                stage_step(unit - base + plain, stage, unit == base + count - 1)
+            else:
+                rows_step(unit, 0, span)
+            return carry
+
+        lax.fori_loop(base, base + count, unit_step, 0)
 
     away = span - tokens
     whole(q_land, q_send_sem).wait()
-    kv_copy.wait_send()
+    on_kv(lambda copy: copy.wait_send())
+
+    @pl.when(lower)
+    def _():
+        help_copy.wait_send()
+
     whole(gq_buf.at[:, :away], gq_send_sem).wait()
     whole(kvp_buf.at[:away], kvp_send_sem).wait()
     whole(out_q, gq_recv_sem).wait()
@@ -328,6 +424,7 @@
             pltpu.VMEM((heads, span, head_dim), bf16),
             pltpu.VMEM(held_kv.shape, bf16),
             pltpu.VMEM((span, 2 * head_dim), bf16),
+            pltpu.VMEM((span * SHIFT // 256 * 16, 2 * head_dim), bf16),
             pltpu.VMEM((span, 2 * head_dim), bf16),
             pltpu.VMEM((heads, span, head_dim), bf16),
             pltpu.VMEM((head_dim, span), bf16),
@@ -337,7 +434,9 @@
             pltpu.VMEM((span, 2 * head_dim), bf16),
             pltpu.VMEM((slots, tokens, 2 * head_dim), bf16),
             dma,
-            dma((heads + 2,)),
+            dma((heads + min(SPLIT, heads),)),
+            dma,
+            dma,
             dma,
             dma,
             dma,

time: 38.4 us -> 36.8 us (0.958)
  the two profiles are of different devices: /device:TPU:26 before, /device:TPU:11 now
where the time goes in v2:
time: 36.8 us; the launch traced here: 36.6 us
  Pallas kernels  36 us (98%)
  between operations  0.64 us (2%)
    pallas_call x1, Pallas kernels, on_device(): pl.pallas_call(functools.partial(kernel, n_section, n_seq, kv_heads, head...  35.1 us
    pallas_call x1, Pallas kernels, on_device(): pl.pallas_call(store_kernel, out_shape=(jax.ShapeDtypeStruct(grad_q.shape...  0.87 us

profile of v2, /device:TPU:11, one launch (start us, length us, event | category | flops | bytes accessed | tf_op | source)
XLA Modules:
  0.0 36.6 jit_solution(1591707261115587583)
XLA Ops:
  0.6 35.1 %shard_map.50 = (bf16[64,4096]{1,0:T(8,128)(2,1)S(1)}, bf16[64,1024]{1,0:T(8,128)(2,1)S(1)}) custom-call(bf16[256,1024]{1,0:T(8,128)(2,1)} %bitcast.5, bf16[256,4,256]{2,1,0:T(4,128)(2,1)} %bitcast.6, bf16[256,1024]{1,0:T(8,128)(2,1)} %bitcast.7), custom_call_target="tpu_custom_call" | custom-call | tf_op jit(solution)/shard_map/pallas_call | solution.py:415
  35.7 0.9 %shard_map.51 = (bf16[64,4096]{1,0:T(8,128)(2,1)}, bf16[64,4,256]{2,1,0:T(4,128)(2,1)}) custom-call(bf16[64,4096]{1,0:T(8,128)(2,1)S(1)} %get-tuple-element.6.grad_q, bf16[64,1024]{1,0:T(8,128)(2,1)S(1)} %get-tuple-element.7.grad_kv), custom_call_target="tpu_custom_call" | custom-call | tf_op jit(solution)/shard_map/pallas_call | solution.py:455
